TPU v7x, 512 devices: a whole 4x8x8 slice. The times are simulated.
512 devices in a mesh: orb: 64 (over z, y), pair: 8 (over x, core).
Axes of the slice: x: 4, y: 8, z: 8, core: 2. Of those that a mesh axis runs over, the one named last changes fastest.
Arguments:
- amplitudes: bfloat16 [4096, 128, 128], P(('orb', 'pair')), may hold values from -6 to 6
- exchange_ints: bfloat16 [4096, 128, 128], P(('orb', 'pair')), may hold values from -6 to 6
- fock_off: bfloat16 [4096, 128, 128], P(('orb', 'pair')), may hold values from -0.6 to 0.6, as said below
- orbital_energies: float32 [4096, 128], P(('orb', 'pair')), may hold values from 0.5 to 4
- occ_shift: float32 [4096], P(('orb', 'pair')), may hold values from 0.5 to 1.5
- far_margins: bfloat16 [32768, 128, 128], P(('orb', 'pair')), may hold values from -0.5 to 0.5
- far_group: int32 [32768, 1], P(('orb', 'pair')), may hold values from 0 to 63; in each aligned block of 64 rows (0 to 63, 64 to 127, ...) at most 2 rows name the same one
- far_pair: int32 [32768], P(('orb', 'pair')), may hold values from 0 to 7
- far_target: int32 [32768], P(('orb', 'pair')), may hold values from 0 to 7
- near_margins: bfloat16 [8192, 128, 128], P(('orb', 'pair')), may hold values from -0.5 to 0.5
- near_column: int32 [8192, 1], P(('orb', 'pair')), may hold values from 0 to 7; in each aligned block of 16 rows (0 to 15, 16 to 31, ...) at most 4 rows name the same one
- near_pair: int32 [8192], P(('orb', 'pair')), may hold values from 0 to 7
- near_target: int32 [8192], P(('orb', 'pair')), may hold values from 0 to 7
Outputs:
- amplitudes_out: float32 [4096, 128, 128], P(('orb', 'pair'))
Inputs may be any that keep to these rules, and one draw needn't show every extreme that they name: `far_group`: among the 64 blocks of one device at most 2 name the same group, and in every draw some device's blocks name some group exactly 2 times. `near_column`: among the 16 blocks of one device at most 4 name the same column, and in every draw some device's blocks name some column exactly 4 times. `fock_off`: each pair's matrix is symmetric with a zero diagonal.
All inputs are finite; a program needn't handle non-finite values.
Results may differ from a plain program's by a relative error of at most 0.0061.
Values may be sent and summed in bfloat16 or wider, within the bound.
A program may use at most 64 MiB of HBM per device.

v0:
```python
import jax
import jax.numpy as jnp
from jax import lax
from jax.sharding import PartitionSpec as P

P_SIZE = 128
ITERS = 2


def slot_layout(destination, groups, capacity):
    blocks = destination.shape[0]
    choose = (destination[:, None] == jnp.arange(groups, dtype=jnp.int32)[None, :]).astype(
        jnp.int32
    )
    earlier = jnp.cumsum(choose, axis=0) - choose
    position = jnp.sum(earlier * choose, axis=1)
    slot_index = destination * capacity + position
    matches = slot_index[None, :] == jnp.arange(groups * capacity, dtype=jnp.int32)[:, None]
    sender = jnp.sum(jnp.where(matches, jnp.arange(blocks, dtype=jnp.int32)[None, :], 0), axis=1)
    filled = jnp.any(matches, axis=1)
    return (slot_index, sender, filled)


def project(margins, incoming):
    halfway = jnp.einsum(
        "bij,bjk->bik", margins, incoming, preferred_element_type=jnp.float32
    ).astype(jnp.bfloat16)
    return jnp.einsum("bik,blk->bil", halfway, margins, preferred_element_type=jnp.float32).astype(
        jnp.bfloat16
    )


def on_device(
    amplitudes,
    exchange_ints,
    fock_off,
    orbital_energies,
    occ_shift,
    far_margins,
    far_group,
    far_pair,
    far_target,
    near_margins,
    near_column,
    near_pair,
    near_target,
):
    orb_count = lax.axis_size("orb")
    pair_count = lax.axis_size("pair")
    local_pairs = amplitudes.shape[0]
    far_owner = far_group[:, 0]
    near_owner = near_column[:, 0]
    far_slot, far_sender, far_filled = slot_layout(
        far_owner, orb_count, 2 * far_owner.shape[0] // orb_count
    )
    near_slot, near_sender, near_filled = slot_layout(
        near_owner, pair_count, 2 * near_owner.shape[0] // pair_count
    )
    targets = jnp.concatenate([far_target, near_target])
    selector = (targets[None, :] == jnp.arange(local_pairs, dtype=jnp.int32)[:, None]).astype(
        jnp.bfloat16
    )
    denominator = (
        orbital_energies[:, :, None] + orbital_energies[:, None, :] + occ_shift[:, None, None]
    )
    current = amplitudes.astype(jnp.float32)
    far_wanted = lax.all_to_all(
        jnp.where(far_filled, far_pair[far_sender], 0),
        "orb",
        split_axis=0,
        concat_axis=0,
        tiled=True,
    )
    near_wanted = lax.all_to_all(
        jnp.where(near_filled, near_pair[near_sender], 0),
        "pair",
        split_axis=0,
        concat_axis=0,
        tiled=True,
    )
    for sweep_index in range(ITERS):
        rounded = current.astype(jnp.bfloat16)
        far_arrived = lax.all_to_all(
            rounded[far_wanted], "orb", split_axis=0, concat_axis=0, tiled=True
        )
        near_arrived = lax.all_to_all(
            rounded[near_wanted], "pair", split_axis=0, concat_axis=0, tiled=True
        )
        far_contrib = project(far_margins, far_arrived[far_slot])
        near_contrib = project(near_margins, near_arrived[near_slot])
        contrib = jnp.concatenate([far_contrib, near_contrib], axis=0)
        block_count = contrib.shape[0]
        couple = jnp.dot(
            selector, contrib.reshape(block_count, -1), preferred_element_type=jnp.float32
        ).reshape(current.shape)
        fock_side = jnp.einsum(
            "pij,pjk->pik", fock_off, rounded, preferred_element_type=jnp.float32
        ) + jnp.einsum("pij,pkj->pik", rounded, fock_off, preferred_element_type=jnp.float32)
        inner_term = jnp.einsum(
            "pij,pjk->pik", rounded, exchange_ints, preferred_element_type=jnp.float32
        ).astype(jnp.bfloat16)
        quadratic = (
            jnp.einsum("pij,pjk->pik", inner_term, rounded, preferred_element_type=jnp.float32)
            / P_SIZE
        )
        residual = (
            exchange_ints.astype(jnp.float32)
            + denominator * current
            + fock_side
            + couple
            + quadratic
        )
        current = current - residual / denominator
    return current


def solution(mesh):
    placed = (
        P(("orb", "pair"), None, None),
        P(("orb", "pair"), None, None),
        P(("orb", "pair"), None, None),
        P(("orb", "pair"), None),
        P(("orb", "pair")),
        P(("orb", "pair"), None, None),
        P(("orb", "pair"), None),
        P(("orb", "pair")),
        P(("orb", "pair")),
        P(("orb", "pair"), None, None),
        P(("orb", "pair"), None),
        P(("orb", "pair")),
        P(("orb", "pair")),
    )
    return jax.shard_map(
        on_device,
        mesh=mesh,
        in_specs=placed,
        out_specs=P(("orb", "pair"), None, None),
        check_vma=False,
    )
```

profile of v0, /device:TPU:44, one launch (start us, length us, event | category | flops | bytes accessed | tf_op | source)
XLA Modules:
  0.0 392.9 jit_solution(3927043270769933664)
XLA Ops:
  0.0 0.9 fusion.34
  0.9 0.8 select_reduce_fusion.3
  1.8 0.7 multiply_add_fusion
  2.6 1.4 gather_fusion.3
  4.0 0.7 select_n.97
  4.7 4.8 %all-to-all-start.2 = ((s32[8,4,1]{1,2,0:T(1,128)}), s32[8,4,1]{1,2,0:T(1,128)S(1)}, u32[]{:S(2)}, u32[]{:S(2)}) async-start(s32[8,4,1]{1,2,0:T(1,128)} %bitcast.11), calls=%async_computation.2 | async-start | bytes 8192 | tf_op jit(solution)/shard_map/all_to_all | solution.py:74
  9.5 0.7 fusion.32
  10.3 0.8 select_reduce_fusion.1
  11.1 0.7 multiply_add_fusion.1
  12.0 1.6 gather_fusion
  13.6 0.8 select_n.91
  14.4 16.1 %all-to-all-start = ((s32[64,2,1]{1,2,0:T(1,128)}), s32[64,2,1]{1,2,0:T(1,128)S(1)}, u32[]{:S(2)}, u32[]{:S(2)}) async-start(s32[64,2,1]{1,2,0:T(1,128)} %bitcast.4), calls=%async_computation | async-start | bytes 65536 | tf_op jit(solution)/shard_map/all_to_all | solution.py:67
  30.5 0.5 broadcast.207
  31.0 0.6 reduce.6
  31.8 1.6 gather_fusion.4
  33.5 4.9 %all-to-all-done = s32[64,2,1]{1,2,0:T(1,128)S(1)} async-done(((s32[64,2,1]{1,2,0:T(1,128)}), s32[64,2,1]{1,2,0:T(1,128)S(1)}, u32[]{:S(2)}, u32[]{:S(2)}) %all-to-all-start) | async-done | bytes 544 | tf_op jit(solution)/shard_map/all_to_all | solution.py:67
  38.3 4.8 %all-to-all-start.3 = ((bf16[32,128,128]{2,1,0:T(8,128)(2,1)}), bf16[32,128,128]{2,1,0:T(8,128)(2,1)S(1)}, u32[]{:S(2)}, u32[]{:S(2)}) async-start(bf16[32,128,128]{2,1,0:T(8,128)(2,1)} %gather_fusion.4), calls=%async_computation.3 | async-start | bytes 2097152 | tf_op jit(solution)/shard_map/all_to_all | solution.py:86
  43.1 0.7 reduce.7
  43.8 0.1 all_to_all.25
  44.0 3.0 gather_fusion.1
  47.0 8.9 %all-to-all-done.3 = bf16[32,128,128]{2,1,0:T(8,128)(2,1)S(1)} async-done(((bf16[32,128,128]{2,1,0:T(8,128)(2,1)}), bf16[32,128,128]{2,1,0:T(8,128)(2,1)S(1)}, u32[]{:S(2)}, u32[]{:S(2)}) %all-to-all-start.3) | async-done | bytes 1048608 | tf_op jit(solution)/shard_map/all_to_all | solution.py:86
  55.9 1.0 copy-done.3
  57.0 9.6 %all-to-all-start.1 = ((bf16[128,128,128]{2,1,0:T(8,128)(2,1)}), bf16[128,128,128]{2,1,0:T(8,128)(2,1)}, u32[]{:S(2)}, u32[]{:S(2)}) async-start(bf16[128,128,128]{2,1,0:T(8,128)(2,1)} %gather_fusion.1), calls=%async_computation.1 | async-start | bytes 8388608 | tf_op jit(solution)/shard_map/all_to_all | solution.py:83
  66.8 2.0 fusion.47
  68.8 2.6 gather_fusion.5
  71.4 1.9 convolution_convert_fusion.2
  73.3 122.9 %all-to-all-done.1 = bf16[128,128,128]{2,1,0:T(8,128)(2,1)} async-done(((bf16[128,128,128]{2,1,0:T(8,128)(2,1)}), bf16[128,128,128]{2,1,0:T(8,128)(2,1)}, u32[]{:S(2)}, u32[]{:S(2)}) %all-to-all-start.1) | async-done | bytes 4194336 | tf_op jit(solution)/shard_map/all_to_all | solution.py:83
  196.2 4.3 %gather_fusion.2 = bf16[64,128,128]{2,1,0:T(8,128)(2,1)} fusion(bf16[128,128,128]{2,1,0:T(8,128)(2,1)} %all-to-all-done.1, s32[1024]{0:T(1024)S(1)} %pad_clamp_fusion.3), kind=kCustom, calls=%fused_computation.2 | custom fusion | bytes 4194560 | tf_op jit(solution)/shard_map/gather | solution.py:89
  200.6 5.8 %fusion.14 = bf16[64,128,128]{2,1,0:T(8,128)(2,1)} fusion(bf16[64,128,128]{2,1,0:T(8,128)(2,1)S(1)} %copy-done, bf16[64,128,128]{2,1,0:T(8,128)(2,1)} %gather_fusion.2), kind=kOutput, calls=%fused_computation.26 | convolution fusion | flops 538968064 | bytes 6291456 | tf_op jit(solution)/shard_map/bik,blk->bil/dot_general | solution.py:28
  206.4 1.8 pad_maximum_fusion
  208.3 1.5 fusion.3
  209.8 1.2 fusion.30
  211.0 2.3 fusion.46
  213.4 1.7 gather_fusion.8
  215.0 6.3 %all-to-all-start.5 = ((bf16[32,128,128]{2,1,0:T(8,128)(2,1)}), bf16[32,128,128]{2,1,0:T(8,128)(2,1)}, u32[]{:S(2)}, u32[]{:S(2)}) async-start(bf16[32,128,128]{2,1,0:T(8,128)(2,1)} %gather_fusion.8), calls=%async_computation.5 | async-start | bytes 2097152 | tf_op jit(solution)/shard_map/all_to_all | solution.py:86
  221.3 3.0 gather_fusion.6
  224.3 9.8 %all-to-all-done.5 = bf16[32,128,128]{2,1,0:T(8,128)(2,1)} async-done(((bf16[32,128,128]{2,1,0:T(8,128)(2,1)}), bf16[32,128,128]{2,1,0:T(8,128)(2,1)}, u32[]{:S(2)}, u32[]{:S(2)}) %all-to-all-start.5) | async-done | bytes 1048608 | tf_op jit(solution)/shard_map/all_to_all | solution.py:86
  234.2 12.7 %all-to-all-start.4 = ((bf16[128,128,128]{2,1,0:T(8,128)(2,1)}), bf16[128,128,128]{2,1,0:T(8,128)(2,1)}, u32[]{:S(2)}, u32[]{:S(2)}) async-start(bf16[128,128,128]{2,1,0:T(8,128)(2,1)} %gather_fusion.6), calls=%async_computation.4 | async-start | bytes 8388608 | tf_op jit(solution)/shard_map/all_to_all | solution.py:83
  246.9 1.1 fusion.48
  248.0 1.1 convolution_multiply_fusion
  249.1 2.7 gather_fusion.9
  251.8 2.8 convolution_convert_fusion
  254.5 123.6 %all-to-all-done.4 = bf16[128,128,128]{2,1,0:T(8,128)(2,1)} async-done(((bf16[128,128,128]{2,1,0:T(8,128)(2,1)}), bf16[128,128,128]{2,1,0:T(8,128)(2,1)}, u32[]{:S(2)}, u32[]{:S(2)}) %all-to-all-start.4) | async-done | bytes 4194336 | tf_op jit(solution)/shard_map/all_to_all | solution.py:83
  378.1 4.3 %gather_fusion.7 = bf16[64,128,128]{2,1,0:T(8,128)(2,1)} fusion(bf16[128,128,128]{2,1,0:T(8,128)(2,1)} %all-to-all-done.4, s32[1024]{0:T(1024)S(1)} %pad_clamp_fusion.3), kind=kCustom, calls=%fused_computation.7 | custom fusion | bytes 4194560 | tf_op jit(solution)/shard_map/gather | solution.py:89
  382.4 5.9 %fusion.17 = bf16[64,128,128]{2,1,0:T(8,128)(2,1)} fusion(bf16[64,128,128]{2,1,0:T(8,128)(2,1)S(1)} %copy-done, bf16[64,128,128]{2,1,0:T(8,128)(2,1)} %gather_fusion.7), kind=kOutput, calls=%fused_computation.27 | convolution fusion | flops 538968064 | bytes 6291456 | tf_op jit(solution)/shard_map/bik,blk->bil/dot_general | solution.py:28
  388.3 1.8 pad_maximum_fusion.1
  390.2 1.5 fusion
  391.7 1.2 fusion.25
  (58 shorter events, 0.8 us)
Async XLA Ops:
  0.0 200.6 %copy-start = (bf16[64,128,128]{2,1,0:T(8,128)(2,1)S(1)}, bf16[64,128,128]{2,1,0:T(8,128)(2,1)}, u32[]{:S(2)}) copy-start(bf16[64,128,128]{2,1,0:T(8,128)(2,1)} %param.18) | copy-start | bytes 6291460
  0.0 31.8 %copy-start.1 = (bf16[8,128,128]{2,1,0:T(8,128)(2,1)S(1)}, bf16[8,128,128]{2,1,0:T(8,128)(2,1)}, u32[]{:S(2)}) copy-start(bf16[8,128,128]{2,1,0:T(8,128)(2,1)} %param.13) | copy-start | bytes 786436
  4.7 9.7 %all-to-all-start.2 = ((s32[8,4,1]{1,2,0:T(1,128)}), s32[8,4,1]{1,2,0:T(1,128)S(1)}, u32[]{:S(2)}, u32[]{:S(2)}) async-start(s32[8,4,1]{1,2,0:T(1,128)} %bitcast.11), calls=%async_computation.2 | async-start | bytes 8192 | tf_op jit(solution)/shard_map/all_to_all | solution.py:74
  14.4 24.0 %all-to-all-start = ((s32[64,2,1]{1,2,0:T(1,128)}), s32[64,2,1]{1,2,0:T(1,128)S(1)}, u32[]{:S(2)}, u32[]{:S(2)}) async-start(s32[64,2,1]{1,2,0:T(1,128)} %bitcast.4), calls=%async_computation | async-start | bytes 65536 | tf_op jit(solution)/shard_map/all_to_all | solution.py:67
  38.3 17.6 %all-to-all-start.3 = ((bf16[32,128,128]{2,1,0:T(8,128)(2,1)}), bf16[32,128,128]{2,1,0:T(8,128)(2,1)S(1)}, u32[]{:S(2)}, u32[]{:S(2)}) async-start(bf16[32,128,128]{2,1,0:T(8,128)(2,1)} %gather_fusion.4), calls=%async_computation.3 | async-start | bytes 2097152 | tf_op jit(solution)/shard_map/all_to_all | solution.py:86
  47.0 19.6 %copy-start.15 = (s32[16]{0:T(128)S(1)}, s32[16]{0:T(128)}, u32[]{:S(2)}) copy-start(s32[16]{0:T(128)} %param.25) | copy-start | bytes 196
  47.0 19.6 %copy-start.16 = (s32[64]{0:T(128)S(1)}, s32[64]{0:T(128)}, u32[]{:S(2)}) copy-start(s32[64]{0:T(128)} %param.21) | copy-start | bytes 772
  47.0 19.7 %copy-start.12 = (s32[64,1]{0,1:T(1,128)S(1)}, s32[64,1]{0,1:T(1,128)}, u32[]{:S(2)}) copy-start(s32[64,1]{0,1:T(1,128)} %param.19) | copy-start | bytes 772
  47.0 19.7 %copy-start.13 = (s32[16,1]{0,1:T(1,128)S(1)}, s32[16,1]{0,1:T(1,128)}, u32[]{:S(2)}) copy-start(s32[16,1]{0,1:T(1,128)} %param.23) | copy-start | bytes 196
  55.9 1.0 copy-start.3
  57.0 139.2 %all-to-all-start.1 = ((bf16[128,128,128]{2,1,0:T(8,128)(2,1)}), bf16[128,128,128]{2,1,0:T(8,128)(2,1)}, u32[]{:S(2)}, u32[]{:S(2)}) async-start(bf16[128,128,128]{2,1,0:T(8,128)(2,1)} %gather_fusion.1), calls=%async_computation.1 | async-start | bytes 8388608 | tf_op jit(solution)/shard_map/all_to_all | solution.py:83
  66.7 4.8 %copy-start.2 = (bf16[16,128,128]{2,1,0:T(8,128)(2,1)S(1)}, bf16[16,128,128]{2,1,0:T(8,128)(2,1)}, u32[]{:S(2)}) copy-start(bf16[16,128,128]{2,1,0:T(8,128)(2,1)} %param.22) | copy-start | bytes 1572868
  208.2 1.6 copy-start.4
  208.2 1.5 copy-start.6
  208.2 1.5 copy-start.7
  208.3 1.5 copy-start.11
  208.3 1.5 copy-start.14
  215.0 19.2 %all-to-all-start.5 = ((bf16[32,128,128]{2,1,0:T(8,128)(2,1)}), bf16[32,128,128]{2,1,0:T(8,128)(2,1)}, u32[]{:S(2)}, u32[]{:S(2)}) async-start(bf16[32,128,128]{2,1,0:T(8,128)(2,1)} %gather_fusion.8), calls=%async_computation.5 | async-start | bytes 2097152 | tf_op jit(solution)/shard_map/all_to_all | solution.py:86
  224.3 23.6 %copy-start.8 = (bf16[8,128,128]{2,1,0:T(8,128)(2,1)S(1)}, bf16[8,128,128]{2,1,0:T(8,128)(2,1)}, u32[]{:S(2)}) copy-start(bf16[8,128,128]{2,1,0:T(8,128)(2,1)} %param.14) | copy-start | bytes 786436
  234.2 143.9 %all-to-all-start.4 = ((bf16[128,128,128]{2,1,0:T(8,128)(2,1)}), bf16[128,128,128]{2,1,0:T(8,128)(2,1)}, u32[]{:S(2)}, u32[]{:S(2)}) async-start(bf16[128,128,128]{2,1,0:T(8,128)(2,1)} %gather_fusion.6), calls=%async_computation.4 | async-start | bytes 8388608 | tf_op jit(solution)/shard_map/all_to_all | solution.py:83
  382.4 5.9 %copy-start.5 = (bf16[16,128,128]{2,1,0:T(8,128)(2,1)S(1)}, bf16[16,128,128]{2,1,0:T(8,128)(2,1)}, u32[]{:S(2)}) copy-start(bf16[16,128,128]{2,1,0:T(8,128)(2,1)} %convolution_convert_fusion) | copy-start | bytes 1572868
  390.2 1.5 copy-start.9
  390.2 1.5 copy-start.10
  390.2 1.5 copy-start.17
where the time goes:
time: 394 us; the launch traced here: 393 us
  waiting for transfers between devices  270 us (69%)
  starting transfers between devices  54.4 us (14%)
  local copies, waits for them, and re-layouts  29.6 us (8%)
  matrix products  28.4 us (7%)
  other arithmetic  10.3 us (3%)
    all_to_all x2, waiting for transfers between devices, on_device(): lax.all_to_all(rounded[far_wanted], 'orb', split_axis=0, concat_axis=0, t...  246 us
    all_to_all x2, starting transfers between devices, on_device(): lax.all_to_all(rounded[far_wanted], 'orb', split_axis=0, concat_axis=0, t...  22.3 us
    all_to_all x2, waiting for transfers between devices, on_device(): lax.all_to_all(rounded[near_wanted], 'pair', split_axis=0, concat_axis=0,...  18.7 us
    dot_general x4, matrix products, project(): jnp.einsum('bik,blk->bil', halfway, margins, preferred_element_type=jnp.f...  16.4 us
    all_to_all x1, starting transfers between devices, on_device(): lax.all_to_all(jnp.where(far_filled, far_pair[far_sender], 0), 'orb', spl...  16.1 us
    all_to_all x2, starting transfers between devices, on_device(): lax.all_to_all(rounded[near_wanted], 'pair', split_axis=0, concat_axis=0,...  11.1 us
    gather x2, local copies, waits for them, and re-layouts, on_device(): far_contrib = project(far_margins, far_arrived[far_slot])  8.66 us
  transfers between devices with their start and end apart: 6, of which 5 were waited for; matrix products, arithmetic and copies ran while one was open for 7% of the time, Pallas kernels for 0%

commit v1 on v0

v1 whole, which is shorter than its diff:
```python
import functools
import math

import jax
import jax.numpy as jnp
from jax import lax
from jax.experimental import pallas as pl
from jax.experimental.pallas import tpu as pltpu
from jax.sharding import PartitionSpec as P

MESH = pl.DeviceIdType.MESH
SIZE = 128
PAIRS = 8
STRIDE = 16
F32 = jnp.float32
BF16 = jnp.bfloat16

ROW_PAIR, ROW_ORDER, ROW_BOUND, ROW_INDEX, NEAR_ORDER, NEAR_SOURCE, NEAR_BOUND = range(7)


def column(row):
    n = row.shape[1]
    diagonal = lax.broadcasted_iota(jnp.int32, (n, n), 0) == lax.broadcasted_iota(
        jnp.int32, (n, n), 1
    )
    return jnp.sum(jnp.where(diagonal, jnp.broadcast_to(row, (n, n)), 0.0), axis=1, keepdims=True)


def plan_kernel(ring, far_ref, near_ref, plan_ref):
    core = lax.rem(lax.axis_index("pair"), 2)
    group = far_ref[0:1, :]
    blocks = group.shape[1]
    shift = ring.bit_length() - 1
    high = lax.shift_right_logical(group, shift)
    low = jnp.bitwise_and(group, ring - 1)
    first = jnp.where(core == 0, high, low).astype(F32)
    second = jnp.where(core == 0, low, high).astype(F32)
    group = group.astype(F32)
    pair = far_ref[1:2, :].astype(F32)
    target = far_ref[2:3, :].astype(F32)
    group_c, first_c, second_c = column(group), column(first), column(second)
    pair_c, target_c = column(pair), column(target)
    here = lax.broadcasted_iota(jnp.int32, (blocks, blocks), 0)
    there = lax.broadcasted_iota(jnp.int32, (blocks, blocks), 1)
    earlier = there < here

    def count(mask):
        return jnp.sum(jnp.where(mask, 1.0, 0.0), axis=1, keepdims=True)

    twin = count((group_c == group) & earlier)
    place = second_c * 2.0 + twin
    slot = first_c * STRIDE + place
    smaller = (target < target_c) | ((target == target_c) & earlier)
    rank = count((first_c == first) & smaller)
    lane = lax.broadcasted_iota(jnp.int32, (blocks, SIZE), 1)
    lane_f = lane.astype(F32)
    number = lax.broadcasted_iota(jnp.int32, (blocks, SIZE), 0).astype(F32)

    def spread(where, value):
        return jnp.sum(jnp.where(where, value, 0.0), axis=0, keepdims=True)

    rows = [
        spread(slot == lane_f, jnp.broadcast_to(pair_c, lane.shape)),
        spread(first_c * STRIDE + rank == lane_f, jnp.broadcast_to(place, lane.shape)),
        spread(
            (first_c == lax.shift_right_logical(lane, 4).astype(F32))
            & (target_c < jnp.bitwise_and(lane, STRIDE - 1).astype(F32)),
            jnp.ones_like(lane_f),
        ),
        spread(slot == lane_f, number),
    ]

    near = near_ref[0:1, :].shape[1]
    source = near_ref[0:1, :].astype(F32) * PAIRS + near_ref[1:2, :].astype(F32)
    goal = near_ref[2:3, :].astype(F32)
    source_c, goal_c = column(source), column(goal)
    before = lax.broadcasted_iota(jnp.int32, (near, near), 1) < lax.broadcasted_iota(
        jnp.int32, (near, near), 0
    )
    near_rank = count((goal < goal_c) | ((goal == goal_c) & before))
    lanes = lax.broadcasted_iota(jnp.int32, (near, SIZE), 1).astype(F32)
    numbers = lax.broadcasted_iota(jnp.int32, (near, SIZE), 0).astype(F32)
    rows += [
        spread(near_rank == lanes, numbers),
        spread(near_rank == lanes, jnp.broadcast_to(source_c, lanes.shape)),
        spread(goal_c < lanes, jnp.ones_like(lanes)),
        jnp.zeros((1, SIZE), F32),
    ]
    for number_of, row in enumerate(rows):
        plan_ref[number_of : number_of + 1, :] = row.astype(jnp.int32)


def contribution(margin, source):
    halfway = jnp.dot(margin, source, preferred_element_type=F32).astype(BF16)
    return lax.dot_general(
        halfway, margin, (((1,), (1,)), ((), ())), preferred_element_type=F32
    ).astype(BF16)


def main_kernel(
    ring,
    columns,
    plan_ref,
    plan_smem,
    amplitudes,
    exchange,
    fock,
    energies,
    shift,
    far,
    near,
    out,
    margins_out,
    margins_in,
    plan_in,
    plans,
    gathered,
    rounded,
    later,
    near_one,
    near_two,
    contrib,
    prefix,
    near_prefix,
    denominator,
    partial_residual,
    state,
    sum_out,
    sum_in,
    margin_sem,
    plan_sem,
    plan_local_sem,
    gather_sem,
    near_sem,
    sum_sem,
):
    half_ring = ring // 2
    half = PAIRS // 2
    orb = lax.axis_index("orb")
    pair = lax.axis_index("pair")
    core = lax.rem(pair, 2)
    x = lax.div(pair, 2)
    high, low = lax.div(orb, ring), lax.rem(orb, ring)
    a = high * (1 - core) + low * core
    b = low * (1 - core) + high * core

    def along_a(step):
        return orb_of(lax.rem(a + (step % ring), ring), b)

    def along_b(step):
        return orb_of(a, lax.rem(b + (step % ring), ring))

    def orb_of(at_a, at_b):
        return (at_a * ring + at_b) * (1 - core) + (at_b * ring + at_a) * core

    def column_of(step):
        return lax.rem(x + (step % columns), columns) * 2 + core

    partner = x * 2 + 1 - core
    sends = []

    def send(src, dst, send_sem, recv_sem, device):
        copy = pltpu.make_async_remote_copy(
            src_ref=src,
            dst_ref=dst,
            send_sem=send_sem,
            recv_sem=recv_sem,
            device_id=device,
            device_id_type=MESH,
        )
        copy.start()
        sends.append(copy)

    def arrived(ref, sem):
        pltpu.make_async_copy(ref, ref, sem).wait()

    barrier = pltpu.get_barrier_semaphore()
    peers = [(along_a(d), pair) for d in range(1, ring)]
    peers += [(along_b(1), pair), (along_b(-1), pair)]
    peers += [(orb, column_of(e)) for e in range(1, columns)]
    peers += [(orb, partner)]
    for peer in peers:
        pl.semaphore_signal(barrier, inc=1, device_id=peer, device_id_type=MESH)

    order = [half_ring]
    for d in range(half_ring - 1, 0, -1):
        order += [d, ring - d]

    def collect(k, destination):
        goal = lax.rem(a + k, ring)

        def one(j, _):
            index = plan_smem[ROW_INDEX, goal * STRIDE + j]
            destination[j] = far[index]
            return 0

        lax.fori_loop(0, 2 * ring, one, 0, unroll=4)

    collect(order[0], margins_out.at[order[0]])
    pl.semaphore_wait(barrier, len(peers))

    def gather_start(turn, own, slots, distance_half):
        for h in range(2):
            part = pl.ds(h * half, half)
            gather_send(turn, own, slots, 1, h, part)

    def gather_send(turn, source, slots, level, h, part, ways=(0, 1)):
        for way in ways:
            if level == half_ring and h != way:
                continue
            number = level if (way == 0 or level == half_ring) else ring - level
            send(
                source.at[part],
                slots[number].at[part],
                gather_sem.at[0, turn, number, h],
                gather_sem.at[1, turn, number, h],
                (along_b(1 if way == 0 else -1), pair),
            )

    def gather_pass(turn, slots, level, h):
        part = pl.ds(h * half, half)
        for way in range(2):
            if level == half_ring:
                if h == way:
                    arrived(slots[level].at[part], gather_sem.at[1, turn, level, h])
                continue
            number = level if way == 0 else ring - level
            arrived(slots[number].at[part], gather_sem.at[1, turn, number, h])
            gather_send(turn, slots[number], slots, level + 1, h, part, (way,))

    def near_rows(at):
        return pl.ds(pl.multiple_of(at * PAIRS, PAIRS), PAIRS)

    def near_start(turn, own, slots):
        for e in range(1, columns):
            send(
                own,
                slots.at[near_rows(pair)],
                near_sem.at[0, turn, e],
                near_sem.at[1, turn, e],
                (orb, column_of(e)),
            )
        send(
            own,
            slots.at[near_rows(pair)],
            near_sem.at[0, turn, columns],
            near_sem.at[1, turn, columns],
            (orb, partner),
        )
        slots[near_rows(pair)] = own[...]

    def near_pass(turn, slots):
        for e in range(1, columns):
            rows = slots.at[near_rows(column_of(-e))]
            arrived(rows, near_sem.at[1, turn, e])
            send(
                rows,
                rows,
                near_sem.at[0, turn, columns + e],
                near_sem.at[1, turn, columns + e],
                (orb, partner),
            )

    def near_finish(turn, slots):
        for e in range(columns):
            came = lax.rem(x + columns - e, columns) * 2 + 1 - core
            arrived(slots.at[near_rows(came)], near_sem.at[1, turn, columns + e])
        blocks = near.shape[0]
        near_prefix[0] = jnp.zeros((SIZE, SIZE), F32)

        def one(k, total):
            margin = near[plan_smem[NEAR_ORDER, k]]
            total = total + contribution(margin, slots[plan_smem[NEAR_SOURCE, k]]).astype(F32)
            near_prefix[k + 1] = total
            return total

        lax.fori_loop(0, blocks, one, jnp.zeros((SIZE, SIZE), F32), unroll=2)

    def local_terms(current, source):
        def one(g, _):
            own = source[g]
            side = jnp.dot(fock[g], own, preferred_element_type=F32) + lax.dot_general(
                own, fock[g], (((1,), (1,)), ((), ())), preferred_element_type=F32
            )
            inner = jnp.dot(own, exchange[g], preferred_element_type=F32).astype(BF16)
            quadratic = jnp.dot(inner, own, preferred_element_type=F32) * (1.0 / SIZE)
            partial_residual[g] = (
                exchange[g].astype(F32)
                + denominator[g] * current[g].astype(F32)
                + side
                + quadratic
            )
            return 0

        lax.fori_loop(0, PAIRS, one, 0)

    def blocks_of(k, g, pairs_ref):
        origin = lax.rem(b + ring - g, ring)
        for twin in range(2):
            place = origin * 2 + twin
            index = plans[k, ROW_PAIR, a * STRIDE + place]
            contrib[k, place] = contribution(margins_in[k, place], pairs_ref(index))

    def prefixes(k):
        prefix[0] = jnp.zeros((SIZE, SIZE), F32)

        def one(j, total):
            total = total + contrib[k, plans[k, ROW_ORDER, a * STRIDE + j]].astype(F32)
            prefix[j + 1] = total
            return total

        lax.fori_loop(0, 2 * ring, one, jnp.zeros((SIZE, SIZE), F32), unroll=4)

    def share(k, t):
        start = plans[k, ROW_BOUND, a * STRIDE + t]
        stop = plans[k, ROW_BOUND, a * STRIDE + t + 1]
        return prefix[stop] - prefix[start]

    def near_share(t):
        start = plan_smem[NEAR_BOUND, t]
        stop = plan_smem[NEAR_BOUND, t + 1]
        return near_prefix[stop] - near_prefix[start]

    def has_input(way, level, h):
        return level + 1 < half_ring or (level + 1 == half_ring and h == way)

    def reduce_send(turn, way, level, k):
        for h in range(2):
            if level == half_ring and h != way:
                continue
            part = pl.ds(h * half, half)
            takes = has_input(way, level, h)
            incoming = sum_in.at[turn, way, level]
            outgoing = sum_out.at[turn, way, level - 1]
            if takes:
                arrived(incoming.at[part], sum_sem.at[1, turn, way, level, h])

            def one(i, _):
                t = h * half + i
                value = share(k, t)
                if takes:
                    value = value + incoming[t].astype(F32)
                outgoing[t] = value.astype(BF16)
                return 0

            lax.fori_loop(0, half, one, 0)
            send(
                outgoing.at[part],
                sum_in.at[turn, way, level - 1].at[part],
                sum_sem.at[0, turn, way, level - 1, h],
                sum_sem.at[1, turn, way, level - 1, h],
                (along_a(1 if way == 0 else -1), pair),
            )

    def reduce_level(turn, level):
        if level == half_ring:
            prefixes(half_ring)
            reduce_send(turn, 0, level, half_ring)
            reduce_send(turn, 1, level, half_ring)
        else:
            prefixes(ring - level)
            reduce_send(turn, 0, level, ring - level)
            prefixes(level)
            reduce_send(turn, 1, level, level)

    def update(turn, current, result):
        prefixes(0)
        for h in range(2):
            part = pl.ds(h * half, half)
            takes = [has_input(way, 0, h) for way in range(2)]
            for way in range(2):
                if takes[way]:
                    arrived(
                        sum_in.at[turn, way, 0].at[part], sum_sem.at[1, turn, way, 0, h]
                    )

            def one(i, _):
                t = h * half + i
                couple = share(0, t) + near_share(t)
                for way in range(2):
                    if takes[way]:
                        couple = couple + sum_in[turn, way, 0, t].astype(F32)
                residual = partial_residual[t] + couple
                new = current[t].astype(F32) - residual / denominator[t]
                result[t] = new
                if turn == 0:
                    rounded[t] = new.astype(BF16)
                return 0

            lax.fori_loop(0, half, one, 0)

    def margin_send(k):
        send(
            plan_ref,
            plan_in.at[k],
            plan_sem.at[0, k],
            plan_sem.at[1, k],
            (along_a(k), pair),
        )
        send(
            margins_out.at[k],
            margins_in.at[k],
            margin_sem.at[0, k],
            margin_sem.at[1, k],
            (along_a(k), pair),
        )

    slots_one = [gathered.at[g] for g in range(ring)]
    slots_two = [rounded] + list(later)
    margin_send(order[0])
    gather_start(0, amplitudes, slots_one, None)
    near_start(0, amplitudes, near_one)
    for k in order[1:]:
        collect(k, margins_out.at[k])
        margin_send(k)
    collect(0, margins_in.at[0])
    gathered[0] = amplitudes[...]
    own_plan = pltpu.make_async_copy(plan_ref, plans.at[0], plan_local_sem.at[0])
    own_plan.start()

    def denominators(g, _):
        row = jnp.broadcast_to(energies[pl.ds(g, 1), :], (SIZE, SIZE))
        denominator[g] = row + row.T + shift[0, g]
        return 0

    lax.fori_loop(0, PAIRS, denominators, 0)
    own_plan.wait()
    for level in range(1, half_ring + 1):
        for h in range(2):
            gather_pass(0, slots_one, level, h)
    local_terms(amplitudes, amplitudes)
    near_pass(0, near_one)
    near_finish(0, near_one)

    def all_groups(k):
        def one(g, _):
            blocks_of(k, g, lambda index: gathered[g, index])
            return 0

        lax.fori_loop(0, ring, one, 0, unroll=2)

    for level in range(half_ring, -1, -1):
        for k in [half_ring] if level == half_ring else [ring - level, level] if level else [0]:
            if k:
                arrived(plan_in.at[k], plan_sem.at[1, k])
                copy = pltpu.make_async_copy(plan_in.at[k], plans.at[k], plan_local_sem.at[k])
                copy.start()
                copy.wait()
                arrived(margins_in.at[k], margin_sem.at[1, k])
            all_groups(k)
        if level:
            reduce_level(0, level)
    update(0, amplitudes, state)

    gather_start(1, rounded, slots_two, None)
    near_start(1, rounded, near_two)

    def group(g):
        def one(k, _):
            blocks_of(k, g, lambda index: slots_two[g][index])
            return 0

        lax.fori_loop(0, ring, one, 0, unroll=2)

    group(0)
    local_terms(state, rounded)
    for level in range(1, half_ring + 1):
        for h in range(2):
            gather_pass(1, slots_two, level, h)
        group(level)
        if level != half_ring:
            group(ring - level)
    near_pass(1, near_two)
    for level in range(half_ring, 0, -1):
        reduce_level(1, level)
        if level == half_ring:
            near_finish(1, near_two)
    update(1, state, out)
    for copy in sends:
        copy.wait_send()


def on_device(
    amplitudes,
    exchange_ints,
    fock_off,
    orbital_energies,
    occ_shift,
    far_margins,
    far_group,
    far_pair,
    far_target,
    near_margins,
    near_column,
    near_pair,
    near_target,
):
    orb_count = lax.axis_size("orb")
    columns = lax.axis_size("pair") // 2
    ring = math.isqrt(orb_count)
    half_ring = ring // 2
    blocks, near_blocks = far_margins.shape[0], near_margins.shape[0]
    vmem = pl.BlockSpec(memory_space=pltpu.VMEM)
    smem = pl.BlockSpec(memory_space=pltpu.SMEM)
    far_table = jnp.stack([far_group[:, 0], far_pair, far_target])
    near_table = jnp.stack([near_column[:, 0], near_pair, near_target])
    plan = pl.pallas_call(
        functools.partial(plan_kernel, ring),
        out_shape=jax.ShapeDtypeStruct((8, SIZE), jnp.int32),
        in_specs=[vmem, vmem],
        out_specs=vmem,
    )(far_table, near_table)
    block = (SIZE, SIZE)
    owned = (PAIRS,) + block
    return pl.pallas_call(
        functools.partial(main_kernel, ring, columns),
        out_shape=jax.ShapeDtypeStruct(owned, F32),
        in_specs=[vmem, smem, vmem, vmem, vmem, vmem, smem, vmem, vmem],
        out_specs=vmem,
        scratch_shapes=[
            pltpu.VMEM((ring, 2 * ring) + block, BF16),
            pltpu.VMEM((ring, 2 * ring) + block, BF16),
            pltpu.VMEM((ring, 8, SIZE), jnp.int32),
            pltpu.SMEM((ring, 8, SIZE), jnp.int32),
            pltpu.VMEM((ring,) + owned, BF16),
            pltpu.VMEM(owned, BF16),
            [pltpu.VMEM(owned, BF16) for _ in range(ring - 1)],
            pltpu.VMEM((2 * columns * PAIRS,) + block, BF16),
            pltpu.VMEM((2 * columns * PAIRS,) + block, BF16),
            pltpu.VMEM((ring, 2 * ring) + block, BF16),
            pltpu.VMEM((2 * ring + 1,) + block, F32),
            pltpu.VMEM((near_blocks + 1,) + block, F32),
            pltpu.VMEM(owned, F32),
            pltpu.VMEM(owned, F32),
            pltpu.VMEM(owned, F32),
            pltpu.VMEM((2, 2, half_ring) + owned, BF16),
            pltpu.VMEM((2, 2, half_ring) + owned, BF16),
            pltpu.SemaphoreType.DMA((2, ring)),
            pltpu.SemaphoreType.DMA((2, ring)),
            pltpu.SemaphoreType.DMA((ring,)),
            pltpu.SemaphoreType.DMA((2, 2, ring, 2)),
            pltpu.SemaphoreType.DMA((2, 2, 2 * columns)),
            pltpu.SemaphoreType.DMA((2, 2, 2, half_ring, 2)),
        ],
        compiler_params=pltpu.CompilerParams(
            collective_id=0, has_side_effects=True, vmem_limit_bytes=60 * 1024 * 1024
        ),
    )(
        plan,
        plan,
        amplitudes,
        exchange_ints,
        fock_off,
        orbital_energies,
        occ_shift.reshape(1, PAIRS),
        far_margins,
        near_margins,
    )


def solution(mesh):
    placed = (
        P(("orb", "pair"), None, None),
        P(("orb", "pair"), None, None),
        P(("orb", "pair"), None, None),
        P(("orb", "pair"), None),
        P(("orb", "pair")),
        P(("orb", "pair"), None, None),
        P(("orb", "pair"), None),
        P(("orb", "pair")),
        P(("orb", "pair")),
        P(("orb", "pair"), None, None),
        P(("orb", "pair"), None),
        P(("orb", "pair")),
        P(("orb", "pair")),
    )
    return jax.shard_map(
        on_device,
        mesh=mesh,
        in_specs=placed,
        out_specs=P(("orb", "pair"), None, None),
        check_vma=False,
    )
```

time: 394 us -> 150 us (0.38)
  the two profiles are of different devices: /device:TPU:44 before, /device:TPU:1 now
where the time goes in v1:
time: 150 us
  Pallas kernels  146 us (97%)
  other arithmetic  2.57 us (2%)
  local copies, waits for them, and re-layouts  1.87 us (1%)
    pallas_call x1, Pallas kernels, on_device(): pl.pallas_call(functools.partial(main_kernel, ring, columns), out_shape=j...  144 us

profile of v1, /device:TPU:1, one launch (start us, length us, event | category | flops | bytes accessed | tf_op | source)
XLA Modules:
  0.0 150.0 jit_solution(14678190358878664300)
XLA Ops:
  0.0 1.3 pad_add_fusion.far_ref
  1.3 1.3 pad_add_fusion.1.near_ref
  2.6 1.5 shard_map.127.plan_ref.plan_smem
  4.1 144.1 %shard_map.128 = f32[8,128,128]{2,1,0:T(8,128)} custom-call(s32[8,128]{1,0:T(8,128)} %shard_map.127.plan_ref.plan_smem, s32[8,128]{1,0:T(8,128)} %shard_map.127.plan_ref.plan_smem, bf16[8,128,128]{2,1,0:T(8,128)(2,1)} %amplitudes.1, bf16[8,128,128]{2,1,0:T(8,128)(2,1)} %exchange.1, bf16[8,128,128]{2,1,0:T(8,128)(2,1)} %fock.1, f32[8,128]{1,0:T(8,128)} %energies.1, ...), custom_call_target="tpu_custom_call" | custom-call | tf_op jit(solution)/shard_map/pallas_call | solution.py:515
  148.2 1.9 %copy.15 = f32[8,128,128]{2,1,0:T(8,128)} copy(f32[8,128,128]{2,1,0:T(8,128)} %shard_map.128) | data formatting | bytes 1048576

commit v2 on v1

v2 whole, which is shorter than its diff:
```python
import functools
import math

import jax
import jax.numpy as jnp
from jax import lax
from jax.experimental import pallas as pl
from jax.experimental.pallas import tpu as pltpu
from jax.sharding import PartitionSpec as P

MESH = pl.DeviceIdType.MESH
SIZE = 128
PAIRS = 8
CHUNKS = 4
CHUNK = PAIRS // CHUNKS
STRIDE = 16
F32 = jnp.float32
BF16 = jnp.bfloat16

ROW_PAIR, ROW_ORDER, ROW_BOUND, ROW_INDEX, NEAR_ORDER, NEAR_SOURCE, NEAR_BOUND = range(7)


def column(row):
    n = row.shape[1]
    diagonal = lax.broadcasted_iota(jnp.int32, (n, n), 0) == lax.broadcasted_iota(
        jnp.int32, (n, n), 1
    )
    return jnp.sum(jnp.where(diagonal, jnp.broadcast_to(row, (n, n)), 0.0), axis=1, keepdims=True)


def plan_kernel(
    ring, group_ref, pair_ref, target_ref, column_ref, near_pair_ref, near_target_ref, plan_ref
):
    core = lax.rem(lax.axis_index("pair"), 2)
    group = group_ref[...]
    blocks = group.shape[1]
    shift = ring.bit_length() - 1
    high = lax.shift_right_logical(group, shift)
    low = jnp.bitwise_and(group, ring - 1)
    first = jnp.where(core == 0, high, low).astype(F32)
    second = jnp.where(core == 0, low, high).astype(F32)
    group = group.astype(F32)
    pair = pair_ref[...].astype(F32)
    target = target_ref[...].astype(F32)
    group_c, first_c, second_c = column(group), column(first), column(second)
    pair_c, target_c = column(pair), column(target)
    here = lax.broadcasted_iota(jnp.int32, (blocks, blocks), 0)
    there = lax.broadcasted_iota(jnp.int32, (blocks, blocks), 1)
    earlier = there < here

    def count(mask):
        return jnp.sum(jnp.where(mask, 1.0, 0.0), axis=1, keepdims=True)

    twin = count((group_c == group) & earlier)
    place = second_c * 2.0 + twin
    slot = first_c * STRIDE + place
    smaller = (target < target_c) | ((target == target_c) & earlier)
    rank = count((first_c == first) & smaller)
    lane = lax.broadcasted_iota(jnp.int32, (blocks, SIZE), 1)
    lane_f = lane.astype(F32)
    number = lax.broadcasted_iota(jnp.int32, (blocks, SIZE), 0).astype(F32)

    def spread(where, value):
        return jnp.sum(jnp.where(where, value, 0.0), axis=0, keepdims=True)

    rows = [
        spread(slot == lane_f, jnp.broadcast_to(pair_c, lane.shape)),
        spread(first_c * STRIDE + rank == lane_f, jnp.broadcast_to(place, lane.shape)),
        spread(
            (first_c == lax.shift_right_logical(lane, 4).astype(F32))
            & (target_c < jnp.bitwise_and(lane, STRIDE - 1).astype(F32)),
            jnp.ones_like(lane_f),
        ),
        spread(slot == lane_f, number),
    ]

    near = column_ref.shape[1]
    source = column_ref[...].astype(F32) * PAIRS + near_pair_ref[...].astype(F32)
    goal = near_target_ref[...].astype(F32)
    source_c, goal_c = column(source), column(goal)
    before = lax.broadcasted_iota(jnp.int32, (near, near), 1) < lax.broadcasted_iota(
        jnp.int32, (near, near), 0
    )
    near_rank = count((goal < goal_c) | ((goal == goal_c) & before))
    lanes = lax.broadcasted_iota(jnp.int32, (near, SIZE), 1).astype(F32)
    numbers = lax.broadcasted_iota(jnp.int32, (near, SIZE), 0).astype(F32)
    rows += [
        spread(near_rank == lanes, numbers),
        spread(near_rank == lanes, jnp.broadcast_to(source_c, lanes.shape)),
        spread(goal_c < lanes, jnp.ones_like(lanes)),
        jnp.zeros((1, SIZE), F32),
    ]
    for number_of, row in enumerate(rows):
        plan_ref[number_of : number_of + 1, :] = row.astype(jnp.int32)


def contribution(margin, source):
    halfway = jnp.dot(margin, source, preferred_element_type=F32).astype(BF16)
    return lax.dot_general(
        halfway, margin, (((1,), (1,)), ((), ())), preferred_element_type=F32
    ).astype(BF16)


def main_kernel(
    ring,
    columns,
    plan_ref,
    plan_smem,
    amplitudes_hbm,
    exchange_hbm,
    fock_hbm,
    energies,
    shift,
    far_hbm,
    near_hbm,
    out,
    amplitudes,
    exchange,
    fock,
    far,
    near,
    margins_out,
    margins_in,
    plan_in,
    plans,
    gathered,
    rounded,
    later,
    near_one,
    near_two,
    contrib,
    prefix,
    near_prefix,
    denominator,
    partial_residual,
    state,
    sum_out,
    sum_in,
    load_sem,
    margin_sem,
    plan_sem,
    plan_local_sem,
    gather_sem,
    near_sem,
    sum_sem,
):
    half_ring = ring // 2
    orb = lax.axis_index("orb")
    pair = lax.axis_index("pair")
    core = lax.rem(pair, 2)
    x = lax.div(pair, 2)
    high, low = lax.div(orb, ring), lax.rem(orb, ring)
    a = high * (1 - core) + low * core
    b = low * (1 - core) + high * core

    def orb_of(at_a, at_b):
        return (at_a * ring + at_b) * (1 - core) + (at_b * ring + at_a) * core

    def along_a(step):
        return orb_of(lax.rem(a + (step % ring), ring), b)

    def along_b(step):
        return orb_of(a, lax.rem(b + (step % ring), ring))

    def column_of(step):
        return lax.rem(x + (step % columns), columns) * 2 + core

    partner = x * 2 + 1 - core

    def send(src, dst, send_sem, recv_sem, device):
        pltpu.make_async_remote_copy(
            src_ref=src,
            dst_ref=dst,
            send_sem=send_sem,
            recv_sem=recv_sem,
            device_id=device,
            device_id_type=MESH,
        ).start()

    def done(ref, sem):
        pltpu.make_async_copy(ref, ref, sem).wait()

    barrier = pltpu.get_barrier_semaphore()
    peers = [(along_a(d), pair) for d in range(1, ring)]
    peers += [(along_b(1), pair), (along_b(-1), pair)]
    peers += [(orb, column_of(e)) for e in range(1, columns)]
    peers += [(orb, partner)]
    for peer in peers:
        pl.semaphore_signal(barrier, inc=1, device_id=peer, device_id_type=MESH)
    loads = [
        pltpu.make_async_copy(source, target, load_sem.at[n])
        for n, (source, target) in enumerate(
            [
                (far_hbm, far),
                (amplitudes_hbm, amplitudes),
                (exchange_hbm, exchange),
                (fock_hbm, fock),
                (near_hbm, near),
            ]
        )
    ]
    for load in loads:
        load.start()

    def collect(k, destination):
        goal = lax.rem(a + k, ring)

        def one(j, _):
            index = plan_smem[ROW_INDEX, goal * STRIDE + j]
            destination[j] = far[index]
            return 0

        lax.fori_loop(0, 2 * ring, one, 0, unroll=4)

    def part(q):
        return pl.ds(q * CHUNK, CHUNK)

    def goes(way, q):
        return q < CHUNKS // 2 if way == 0 else q >= CHUNKS // 2

    def when(condition, body):
        if isinstance(condition, bool):
            if condition:
                body()
        else:
            pl.when(condition)(body)

    def gather_send(turn, source, slots, level, q, way):
        number = level if (way == 0 or level == half_ring) else ring - level

        def go():
            send(
                source.at[part(q)],
                slots[number].at[part(q)],
                gather_sem.at[0, turn, number, q],
                gather_sem.at[1, turn, number, q],
                (along_b(1 if way == 0 else -1), pair),
            )

        if level == half_ring:
            when(goes(way, q), go)
        else:
            go()

    def gather_pass(turn, slots, level, q):
        for way in range(2):
            number = level if way == 0 else ring - level
            done(slots[number].at[part(q)], gather_sem.at[1, turn, number, q])
            gather_send(turn, slots[number], slots, level + 1, q, way)

    def gather_levels(turn, slots, work):
        for level in range(1, half_ring):

            def one(q, _):
                gather_pass(turn, slots, level, q)
                work(level, q)
                return 0

            lax.fori_loop(0, CHUNKS, one, 0)

        def last(q, _):
            for at in (q, q + CHUNKS // 2):
                done(slots[half_ring].at[part(at)], gather_sem.at[1, turn, half_ring, at])
                work(half_ring, at)
            return 0

        lax.fori_loop(0, CHUNKS // 2, last, 0)

    def near_rows(at):
        return pl.ds(pl.multiple_of(at * PAIRS, PAIRS), PAIRS)

    def near_start(turn, own, slots):
        for e in range(1, columns):
            send(
                own,
                slots.at[near_rows(pair)],
                near_sem.at[0, turn, e],
                near_sem.at[1, turn, e],
                (orb, column_of(e)),
            )
        send(
            own,
            slots.at[near_rows(pair)],
            near_sem.at[0, turn, columns],
            near_sem.at[1, turn, columns],
            (orb, partner),
        )
        slots[near_rows(pair)] = own[...]

    def near_pass(turn, slots):
        for e in range(1, columns):
            rows = slots.at[near_rows(column_of(-e))]
            done(rows, near_sem.at[1, turn, e])
            send(
                rows,
                rows,
                near_sem.at[0, turn, columns + e],
                near_sem.at[1, turn, columns + e],
                (orb, partner),
            )

    def near_finish(turn, slots):
        for e in range(columns):
            came = lax.rem(x + columns - e, columns) * 2 + 1 - core
            done(slots.at[near_rows(came)], near_sem.at[1, turn, columns + e])
        blocks = near.shape[0]
        near_prefix[0] = jnp.zeros((SIZE, SIZE), F32)

        def one(k, total):
            margin = near[plan_smem[NEAR_ORDER, k]]
            total = total + contribution(margin, slots[plan_smem[NEAR_SOURCE, k]]).astype(F32)
            near_prefix[k + 1] = total
            return total

        lax.fori_loop(0, blocks, one, jnp.zeros((SIZE, SIZE), F32), unroll=4)

    def local_term(current, source, g):
        own = source[g]
        side = jnp.dot(fock[g], own, preferred_element_type=F32) + lax.dot_general(
            own, fock[g], (((1,), (1,)), ((), ())), preferred_element_type=F32
        )
        inner = jnp.dot(own, exchange[g], preferred_element_type=F32).astype(BF16)
        quadratic = jnp.dot(inner, own, preferred_element_type=F32) * (1.0 / SIZE)
        partial_residual[g] = (
            exchange[g].astype(F32)
            + denominator[g] * current[g].astype(F32)
            + side
            + quadratic
        )

    def block_of(k, place, source):
        index = plans[k, ROW_PAIR, a * STRIDE + place]
        contrib[k, place] = contribution(margins_in[k, place], source(index))

    def prefixes(k, bank):
        prefix[bank, 0] = jnp.zeros((SIZE, SIZE), F32)

        def one(j, total):
            total = total + contrib[k, plans[k, ROW_ORDER, a * STRIDE + j]].astype(F32)
            prefix[bank, j + 1] = total
            return total

        lax.fori_loop(0, 2 * ring, one, jnp.zeros((SIZE, SIZE), F32), unroll=4)

    def share(k, bank, t):
        start = plans[k, ROW_BOUND, a * STRIDE + t]
        stop = plans[k, ROW_BOUND, a * STRIDE + t + 1]
        return prefix[bank, stop] - prefix[bank, start]

    def near_share(t):
        start = plan_smem[NEAR_BOUND, t]
        stop = plan_smem[NEAR_BOUND, t + 1]
        return near_prefix[stop] - near_prefix[start]

    def incoming(turn, way, level, q):
        def go():
            done(sum_in.at[turn, way, level].at[part(q)], sum_sem.at[1, turn, way, level, q])

        if level + 1 < half_ring:
            go()
        elif level + 1 == half_ring:
            when(goes(way, q), go)

    def added(turn, way, level, q, t, value):
        if level + 1 > half_ring:
            return value
        more = value + sum_in[turn, way, level, t].astype(F32)
        if level + 1 < half_ring:
            return more
        return jnp.where(goes(way, q), more, value)

    def reduce_send(turn, way, level, k, bank, q):
        incoming(turn, way, level, q)
        for i in range(CHUNK):
            t = q * CHUNK + i
            value = added(turn, way, level, q, t, share(k, bank, t))
            sum_out[turn, way, level - 1, t] = value.astype(BF16)
        send(
            sum_out.at[turn, way, level - 1].at[part(q)],
            sum_in.at[turn, way, level - 1].at[part(q)],
            sum_sem.at[0, turn, way, level - 1, q],
            sum_sem.at[1, turn, way, level - 1, q],
            (along_a(1 if way == 0 else -1), pair),
        )

    def reduce_level(turn, level):
        if level == half_ring:
            prefixes(half_ring, 0)

            def one(q, _):
                reduce_send(turn, 0, level, half_ring, 0, q)
                reduce_send(turn, 1, level, half_ring, 0, q + CHUNKS // 2)
                return 0

            lax.fori_loop(0, CHUNKS // 2, one, 0)
        else:
            prefixes(ring - level, 0)
            prefixes(level, 1)

            def two(q, _):
                reduce_send(turn, 0, level, ring - level, 0, q)
                reduce_send(turn, 1, level, level, 1, q)
                return 0

            lax.fori_loop(0, CHUNKS, two, 0)

    def update(turn, current, result, after):
        prefixes(0, 0)

        def one(q, _):
            for way in range(2):
                incoming(turn, way, 0, q)
            for i in range(CHUNK):
                t = q * CHUNK + i
                couple = share(0, 0, t) + near_share(t)
                for way in range(2):
                    couple = added(turn, way, 0, q, t, couple)
                residual = partial_residual[t] + couple
                new = current[t].astype(F32) - residual / denominator[t]
                result[t] = new
                if turn == 0:
                    rounded[t] = new.astype(BF16)
            after(q)
            return 0

        lax.fori_loop(0, CHUNKS, one, 0)

    slots_one = [gathered.at[g] for g in range(ring)]
    slots_two = [rounded] + list(later)
    levels = [[half_ring]] + [[ring - d, d] for d in range(half_ring - 1, 0, -1)]
    halves = [pl.ds(h * ring, ring) for h in range(2)]

    def margin_send(k):
        for h in range(2):
            send(
                margins_out.at[k].at[halves[h]],
                margins_in.at[k].at[halves[h]],
                margin_sem.at[0, k, h],
                margin_sem.at[1, k, h],
                (along_a(k), pair),
            )

    loads[0].wait()
    collect(half_ring, margins_out.at[half_ring])
    pl.semaphore_wait(barrier, len(peers))
    for k in levels[0]:
        margin_send(k)
    loads[1].wait()
    for q in range(CHUNKS):
        for way in range(2):
            gather_send(0, amplitudes, slots_one, 1, q, way)
    for k in range(1, ring):
        send(plan_ref, plan_in.at[k], plan_sem.at[0, k], plan_sem.at[1, k], (along_a(k), pair))
    for group in levels[1:]:
        for k in group:
            collect(k, margins_out.at[k])
            if group is levels[1]:
                margin_send(k)
    near_start(0, amplitudes, near_one)
    collect(0, margins_in.at[0])
    gathered[0] = amplitudes[...]

    def denominators(g, _):
        row = jnp.broadcast_to(energies[pl.ds(g, 1), :], (SIZE, SIZE))
        denominator[g] = row + row.T + shift[0, g]
        return 0

    lax.fori_loop(0, PAIRS, denominators, 0)
    loads[2].wait()
    loads[3].wait()
    loads[4].wait()

    def first_work(level, q):
        if level == 1:
            for i in range(CHUNK):
                local_term(amplitudes, amplitudes, q * CHUNK + i)

    if half_ring == 1:
        for q in range(CHUNKS):
            first_work(1, q)
        gather_levels(0, slots_one, lambda level, q: None)
    else:
        gather_levels(0, slots_one, first_work)
    near_pass(0, near_one)
    copies = []
    for k in range(ring):
        if k:
            done(plan_in.at[k], plan_sem.at[1, k])
        copies.append(
            pltpu.make_async_copy(plan_in.at[k] if k else plan_ref, plans.at[k], plan_local_sem.at[k])
        )
        copies[-1].start()
    for copy in copies:
        copy.wait()

    def half_target(k, h):
        for i in range(half_ring):
            origin = h * half_ring + i
            g = lax.rem(b + ring - origin, ring)
            for twin in range(2):
                block_of(k, origin * 2 + twin, lambda index: gathered[g, index])

    def target(k):
        for h in range(2):
            if not isinstance(k, int) or k:
                done(margins_in.at[k].at[halves[h]], margin_sem.at[1, k, h])
            half_target(k, h)

    target(0)
    near_finish(0, near_one)
    for n, group in enumerate(levels):
        if len(group) == 1:
            target(group[0])
        else:
            level = group[1]
            lax.fori_loop(
                0, 2, lambda n, _: (target(ring - level - n * (ring - 2 * level)), 0)[1], 0
            )
        reduce_level(0, half_ring - n)
        if n + 2 < len(levels):
            for k in levels[n + 2]:
                margin_send(k)

    def spread(q):
        for way in range(2):
            gather_send(1, rounded, slots_two, 1, q, way)

    update(0, amplitudes, state, spread)

    near_start(1, rounded, near_two)
    share_of = ring // CHUNKS

    def blocks_at(g, k):
        origin = lax.rem(b + ring - g, ring)
        for twin in range(2):
            block_of(k, origin * 2 + twin, lambda index: slots_two[g][index])

    def second_work(level, q):
        if level == 1:
            for i in range(CHUNK):
                local_term(state, rounded, q * CHUNK + i)
        for i in range(share_of):
            k = q * share_of + i
            blocks_at(level - 1, k)
            if level > 1:
                blocks_at(ring - level + 1, k)

    gather_levels(1, slots_two, second_work)
    near_pass(1, near_two)
    for n, group in enumerate(levels):
        for k in group:
            blocks_at(half_ring, k)
        reduce_level(1, half_ring - n)
        if n == 0:
            near_finish(1, near_two)
    blocks_at(half_ring, 0)
    update(1, state, out, lambda q: None)

    for k in range(1, ring):
        done(plan_ref, plan_sem.at[0, k])
        for h in range(2):
            done(margins_out.at[k].at[halves[h]], margin_sem.at[0, k, h])
    for turn, slots, near_slots in ((0, slots_one, near_one), (1, slots_two, near_two)):
        for number in range(1, ring):
            for q in range(CHUNKS):
                done(slots[number].at[part(q)], gather_sem.at[0, turn, number, q])
        for e in range(1, 2 * columns):
            done(near_slots.at[pl.ds(0, PAIRS)], near_sem.at[0, turn, e])
        for way in range(2):
            for level in range(half_ring):
                for q in range(CHUNKS):
                    if level + 1 < half_ring or goes(way, q):
                        done(
                            sum_out.at[turn, way, level].at[part(q)],
                            sum_sem.at[0, turn, way, level, q],
                        )


def on_device(
    amplitudes,
    exchange_ints,
    fock_off,
    orbital_energies,
    occ_shift,
    far_margins,
    far_group,
    far_pair,
    far_target,
    near_margins,
    near_column,
    near_pair,
    near_target,
):
    orb_count = lax.axis_size("orb")
    columns = lax.axis_size("pair") // 2
    ring = math.isqrt(orb_count)
    half_ring = ring // 2
    blocks, near_blocks = far_margins.shape[0], near_margins.shape[0]
    vmem = pl.BlockSpec(memory_space=pltpu.VMEM)
    smem = pl.BlockSpec(memory_space=pltpu.SMEM)
    hbm = pl.BlockSpec(memory_space=pl.ANY)
    plan = pl.pallas_call(
        functools.partial(plan_kernel, ring),
        out_shape=jax.ShapeDtypeStruct((8, SIZE), jnp.int32),
        in_specs=[vmem] * 6,
        out_specs=vmem,
    )(
        far_group.reshape(1, blocks),
        far_pair.reshape(1, blocks),
        far_target.reshape(1, blocks),
        near_column.reshape(1, near_blocks),
        near_pair.reshape(1, near_blocks),
        near_target.reshape(1, near_blocks),
    )
    block = (SIZE, SIZE)
    owned = (PAIRS,) + block
    return pl.pallas_call(
        functools.partial(main_kernel, ring, columns),
        out_shape=jax.ShapeDtypeStruct(owned, F32),
        in_specs=[vmem, smem, hbm, hbm, hbm, vmem, smem, hbm, hbm],
        out_specs=vmem,
        scratch_shapes=[
            pltpu.VMEM(owned, BF16),
            pltpu.VMEM(owned, BF16),
            pltpu.VMEM(owned, BF16),
            pltpu.VMEM((blocks,) + block, BF16),
            pltpu.VMEM((near_blocks,) + block, BF16),
            pltpu.VMEM((ring, 2 * ring) + block, BF16),
            pltpu.VMEM((ring, 2 * ring) + block, BF16),
            pltpu.VMEM((ring, 8, SIZE), jnp.int32),
            pltpu.SMEM((ring, 8, SIZE), jnp.int32),
            pltpu.VMEM((ring,) + owned, BF16),
            pltpu.VMEM(owned, BF16),
            [pltpu.VMEM(owned, BF16) for _ in range(ring - 1)],
            pltpu.VMEM((2 * columns * PAIRS,) + block, BF16),
            pltpu.VMEM((2 * columns * PAIRS,) + block, BF16),
            pltpu.VMEM((ring, 2 * ring) + block, BF16),
            pltpu.VMEM((2, 2 * ring + 1) + block, F32),
            pltpu.VMEM((near_blocks + 1,) + block, F32),
            pltpu.VMEM(owned, F32),
            pltpu.VMEM(owned, F32),
            pltpu.VMEM(owned, F32),
            pltpu.VMEM((2, 2, half_ring) + owned, BF16),
            pltpu.VMEM((2, 2, half_ring) + owned, BF16),
            pltpu.SemaphoreType.DMA((5,)),
            pltpu.SemaphoreType.DMA((2, ring, 2)),
            pltpu.SemaphoreType.DMA((2, ring)),
            pltpu.SemaphoreType.DMA((ring,)),
            pltpu.SemaphoreType.DMA((2, 2, ring, CHUNKS)),
            pltpu.SemaphoreType.DMA((2, 2, 2 * columns)),
            pltpu.SemaphoreType.DMA((2, 2, 2, half_ring, CHUNKS)),
        ],
        compiler_params=pltpu.CompilerParams(
            collective_id=0, has_side_effects=True, vmem_limit_bytes=60 * 1024 * 1024
        ),
    )(
        plan,
        plan,
        amplitudes,
        exchange_ints,
        fock_off,
        orbital_energies,
        occ_shift.reshape(1, PAIRS),
        far_margins,
        near_margins,
    )


def solution(mesh):
    placed = (
        P(("orb", "pair"), None, None),
        P(("orb", "pair"), None, None),
        P(("orb", "pair"), None, None),
        P(("orb", "pair"), None),
        P(("orb", "pair")),
        P(("orb", "pair"), None, None),
        P(("orb", "pair"), None),
        P(("orb", "pair")),
        P(("orb", "pair")),
        P(("orb", "pair"), None, None),
        P(("orb", "pair"), None),
        P(("orb", "pair")),
        P(("orb", "pair")),
    )
    return jax.shard_map(
        on_device,
        mesh=mesh,
        in_specs=placed,
        out_specs=P(("orb", "pair"), None, None),
        check_vma=False,
    )
```

time: 150 us -> 136 us (0.907)
  Pallas kernels: 146 us -> 133 us
  other arithmetic: 2.57 us -> 0 us
    pallas_call x1, Pallas kernels: 144 us -> 131 us  [on_device(): pl.pallas_call(functools.partial(main_kernel, ring, columns), out_shape=j...]
    another operation x2 -> x0, other arithmetic: 2.57 us -> none  [the longest x1 1.29 us: on_device(): far_table = jnp.stack([far_group[:, 0], far_pair, far_target])]
where the time goes in v2:
time: 136 us; the launch traced here: 135 us
  Pallas kernels  133 us (98%)
  local copies, waits for them, and re-layouts  1.87 us (1%)
    pallas_call x1, Pallas kernels, on_device(): pl.pallas_call(functools.partial(main_kernel, ring, columns), out_shape=j...  131 us

profile of v2, /device:TPU:1, one launch (start us, length us, event | category | flops | bytes accessed | tf_op | source)
XLA Modules:
  0.0 134.6 jit_solution(8370634309903740101)
XLA Ops:
  0.0 1.5 %shard_map.127.plan_ref.plan_smem = s32[8,128]{1,0:T(8,128)} custom-call(s32[1,64]{1,0:T(1,128)} %bitcast.8, s32[1,64]{1,0:T(1,128)} %bitcast.9, s32[1,64]{1,0:T(1,128)} %bitcast.10, s32[1,16]{1,0:T(1,128)} %bitcast.11, s32[1,16]{1,0:T(1,128)} %bitcast.12, s32[1,16]{1,0:T(1,128)} %bitcast.13), custom_call_target="tpu_custom_call" | custom-call | tf_op jit(solution)/shard_map/pallas_call | solution.py:602
  1.5 131.1 %shard_map.128 = f32[8,128,128]{2,1,0:T(8,128)} custom-call(s32[8,128]{1,0:T(8,128)} %shard_map.127.plan_ref.plan_smem, s32[8,128]{1,0:T(8,128)} %shard_map.127.plan_ref.plan_smem, bf16[8,128,128]{2,1,0:T(8,128)(2,1)} %amplitudes_hbm.1, bf16[8,128,128]{2,1,0:T(8,128)(2,1)} %exchange_hbm.1, bf16[8,128,128]{2,1,0:T(8,128)(2,1)} %fock_hbm.1, ...), custom_call_target="tpu_custom_call" | custom-call | tf_op jit(solution)/shard_map/pallas_call | solution.py:617
  132.7 1.9 %copy.15 = f32[8,128,128]{2,1,0:T(8,128)} copy(f32[8,128,128]{2,1,0:T(8,128)} %shard_map.128) | data formatting | bytes 1048576

commit v3 on v2

--- a/solution.py
+++ b/solution.py
@@ -65,11 +65,17 @@
 
     rows = [
         spread(slot == lane_f, jnp.broadcast_to(pair_c, lane.shape)),
-        spread(first_c * STRIDE + rank == lane_f, jnp.broadcast_to(place, lane.shape)),
-        spread(
-            (first_c == lax.shift_right_logical(lane, 4).astype(F32))
-            & (target_c < jnp.bitwise_and(lane, STRIDE - 1).astype(F32)),
-            jnp.ones_like(lane_f),
+        jnp.minimum(
+            spread(first_c * STRIDE + rank == lane_f, jnp.broadcast_to(place, lane.shape)),
+            2.0 * ring - 1.0,
+        ),
+        jnp.minimum(
+            spread(
+                (first_c == lax.shift_right_logical(lane, 4).astype(F32))
+                & (target_c < jnp.bitwise_and(lane, STRIDE - 1).astype(F32)),
+                jnp.ones_like(lane_f),
+            ),
+            2.0 * ring,
         ),
         spread(slot == lane_f, number),
     ]
@@ -182,7 +188,7 @@
 
     barrier = pltpu.get_barrier_semaphore()
     peers = [(along_a(d), pair) for d in range(1, ring)]
-    peers += [(along_b(1), pair), (along_b(-1), pair)]
+    peers += [(along_b(step), pair) for step in (1, -1, 2, -2)]
     peers += [(orb, column_of(e)) for e in range(1, columns)]
     peers += [(orb, partner)]
     for peer in peers:
@@ -201,6 +207,8 @@
     ]
     for load in loads:
         load.start()
+    for load in loads:
+        load.wait()
 
     def collect(k, destination):
         goal = lax.rem(a + k, ring)
@@ -226,9 +234,8 @@
             pl.when(condition)(body)
 
     def gather_send(turn, source, slots, level, q, way):
-        number = level if (way == 0 or level == half_ring) else ring - level
-
-        def go():
+        if level < half_ring:
+            number = level if way == 0 else ring - level
             send(
                 source.at[part(q)],
                 slots[number].at[part(q)],
@@ -237,10 +244,17 @@
                 (along_b(1 if way == 0 else -1), pair),
             )
 
-        if level == half_ring:
-            when(goes(way, q), go)
-        else:
-            go()
+        def opposite():
+            send(
+                source.at[part(q)],
+                slots[half_ring].at[part(q)],
+                gather_sem.at[0, turn, half_ring, q],
+                gather_sem.at[1, turn, half_ring, q],
+                (along_b(2 if way == 0 else -2), pair),
+            )
+
+        if level == half_ring - 1:
+            when(goes(way, q), opposite)
 
     def gather_pass(turn, slots, level, q):
         for way in range(2):
@@ -248,8 +262,10 @@
             done(slots[number].at[part(q)], gather_sem.at[1, turn, number, q])
             gather_send(turn, slots[number], slots, level + 1, q, way)
 
-    def gather_levels(turn, slots, work):
+    def gather_levels(turn, slots, work, between=None):
         for level in range(1, half_ring):
+            if level == 2 and between is not None:
+                between()
 
             def one(q, _):
                 gather_pass(turn, slots, level, q)
@@ -257,6 +273,8 @@
                 return 0
 
             lax.fori_loop(0, CHUNKS, one, 0)
+        if half_ring == 2 and between is not None:
+            between()
 
         def last(q, _):
             for at in (q, q + CHUNKS // 2):
@@ -353,21 +371,21 @@
         return near_prefix[stop] - near_prefix[start]
 
     def incoming(turn, way, level, q):
-        def go():
-            done(sum_in.at[turn, way, level].at[part(q)], sum_sem.at[1, turn, way, level, q])
-
-        if level + 1 < half_ring:
-            go()
-        elif level + 1 == half_ring:
-            when(goes(way, q), go)
+        def wait(slot):
+            done(sum_in.at[turn, way, slot].at[part(q)], sum_sem.at[1, turn, way, slot, q])
+
+        if level < half_ring - 1:
+            wait(level)
+        if level == half_ring - 2:
+            when(goes(way, q), lambda: wait(half_ring - 1))
 
     def added(turn, way, level, q, t, value):
-        if level + 1 > half_ring:
-            return value
-        more = value + sum_in[turn, way, level, t].astype(F32)
-        if level + 1 < half_ring:
-            return more
-        return jnp.where(goes(way, q), more, value)
+        if level < half_ring - 1:
+            value = value + sum_in[turn, way, level, t].astype(F32)
+        if level == half_ring - 2:
+            more = value + sum_in[turn, way, half_ring - 1, t].astype(F32)
+            value = jnp.where(goes(way, q), more, value)
+        return value
 
     def reduce_send(turn, way, level, k, bank, q):
         incoming(turn, way, level, q)
@@ -380,7 +398,7 @@
             sum_in.at[turn, way, level - 1].at[part(q)],
             sum_sem.at[0, turn, way, level - 1, q],
             sum_sem.at[1, turn, way, level - 1, q],
-            (along_a(1 if way == 0 else -1), pair),
+            (along_a((2 if level == half_ring else 1) * (1 if way == 0 else -1)), pair),
         )
 
     def reduce_level(turn, level):
@@ -440,12 +458,8 @@
                 (along_a(k), pair),
             )
 
-    loads[0].wait()
     collect(half_ring, margins_out.at[half_ring])
     pl.semaphore_wait(barrier, len(peers))
-    for k in levels[0]:
-        margin_send(k)
-    loads[1].wait()
     for q in range(CHUNKS):
         for way in range(2):
             gather_send(0, amplitudes, slots_one, 1, q, way)
@@ -454,8 +468,6 @@
     for group in levels[1:]:
         for k in group:
             collect(k, margins_out.at[k])
-            if group is levels[1]:
-                margin_send(k)
     near_start(0, amplitudes, near_one)
     collect(0, margins_in.at[0])
     gathered[0] = amplitudes[...]
@@ -466,21 +478,18 @@
         return 0
 
     lax.fori_loop(0, PAIRS, denominators, 0)
-    loads[2].wait()
-    loads[3].wait()
-    loads[4].wait()
+
+    def margins_leave():
+        for group in levels:
+            for k in group:
+                margin_send(k)
 
     def first_work(level, q):
         if level == 1:
             for i in range(CHUNK):
                 local_term(amplitudes, amplitudes, q * CHUNK + i)
 
-    if half_ring == 1:
-        for q in range(CHUNKS):
-            first_work(1, q)
-        gather_levels(0, slots_one, lambda level, q: None)
-    else:
-        gather_levels(0, slots_one, first_work)
+    gather_levels(0, slots_one, first_work, margins_leave)
     near_pass(0, near_one)
     copies = []
     for k in range(ring):
@@ -517,9 +526,6 @@
                 0, 2, lambda n, _: (target(ring - level - n * (ring - 2 * level)), 0)[1], 0
             )
         reduce_level(0, half_ring - n)
-        if n + 2 < len(levels):
-            for k in levels[n + 2]:
-                margin_send(k)
 
     def spread(q):
         for way in range(2):
@@ -599,19 +605,20 @@
     vmem = pl.BlockSpec(memory_space=pltpu.VMEM)
     smem = pl.BlockSpec(memory_space=pltpu.SMEM)
     hbm = pl.BlockSpec(memory_space=pl.ANY)
-    plan = pl.pallas_call(
-        functools.partial(plan_kernel, ring),
-        out_shape=jax.ShapeDtypeStruct((8, SIZE), jnp.int32),
-        in_specs=[vmem] * 6,
-        out_specs=vmem,
-    )(
+    tables = [
         far_group.reshape(1, blocks),
         far_pair.reshape(1, blocks),
         far_target.reshape(1, blocks),
         near_column.reshape(1, near_blocks),
         near_pair.reshape(1, near_blocks),
         near_target.reshape(1, near_blocks),
-    )
+    ]
+    plan = pl.pallas_call(
+        functools.partial(plan_kernel, ring),
+        out_shape=jax.ShapeDtypeStruct((8, SIZE), jnp.int32),
+        in_specs=[vmem] * 6,
+        out_specs=vmem,
+    )(*tables)
     block = (SIZE, SIZE)
     owned = (PAIRS,) + block
     return pl.pallas_call(

time: 136 us -> 130 us (0.956); the launches traced: 135 us -> 130 us
  Pallas kernels: 133 us -> 128 us
    pallas_call x1, Pallas kernels: 131 us -> 127 us  [on_device(): pl.pallas_call(functools.partial(main_kernel, ring, columns), out_shape=j...]
where the time goes in v3:
time: 130 us
  Pallas kernels  128 us (98%)
  local copies, waits for them, and re-layouts  1.87 us (1%)
    pallas_call x1, Pallas kernels, on_device(): pl.pallas_call(functools.partial(main_kernel, ring, columns), out_shape=j...  127 us

profile of v3, /device:TPU:1, one launch (start us, length us, event | category | flops | bytes accessed | tf_op | source)
XLA Modules:
  0.0 130.2 jit_solution(14623069474144736436)
XLA Ops:
  0.0 1.5 %shard_map.127.plan_ref.plan_smem = s32[8,128]{1,0:T(8,128)} custom-call(s32[1,64]{1,0:T(1,128)} %bitcast.8, s32[1,64]{1,0:T(1,128)} %bitcast.9, s32[1,64]{1,0:T(1,128)} %bitcast.10, s32[1,16]{1,0:T(1,128)} %bitcast.11, s32[1,16]{1,0:T(1,128)} %bitcast.12, s32[1,16]{1,0:T(1,128)} %bitcast.13), custom_call_target="tpu_custom_call" | custom-call | tf_op jit(solution)/shard_map/pallas_call | solution.py:616
  1.5 126.8 %shard_map.128 = f32[8,128,128]{2,1,0:T(8,128)} custom-call(s32[8,128]{1,0:T(8,128)} %shard_map.127.plan_ref.plan_smem, s32[8,128]{1,0:T(8,128)} %shard_map.127.plan_ref.plan_smem, bf16[8,128,128]{2,1,0:T(8,128)(2,1)} %amplitudes_hbm.1, bf16[8,128,128]{2,1,0:T(8,128)(2,1)} %exchange_hbm.1, bf16[8,128,128]{2,1,0:T(8,128)(2,1)} %fock_hbm.1, ...), custom_call_target="tpu_custom_call" | custom-call | tf_op jit(solution)/shard_map/pallas_call | solution.py:624
  128.3 1.9 %copy.15 = f32[8,128,128]{2,1,0:T(8,128)} copy(f32[8,128,128]{2,1,0:T(8,128)} %shard_map.128) | data formatting | bytes 1048576
